TPU v7x, 128 devices: a whole 4x4x4 slice. The times are simulated.
128 devices in a mesh: lat: 8 (over x, core), lon: 16 (over y, z).
Axes of the slice: x: 4, y: 4, z: 4, core: 2. Of those that a mesh axis runs over, the one named last changes fastest.
Arguments:
- spectra: bfloat16 [393216, 616], P(('lat', 'lon')), may hold values from -6 to 6
- block_target: int32 [3072], P(('lat', 'lon')), may hold values from 0 to 15, as said below
- block_patch: int32 [3072], P(('lat', 'lon')), may hold values from 0 to 11
- block_kernel: int32 [3072], P(('lat', 'lon')), may hold values from 0 to 15
- encoder_weight: bfloat16 [616, 512], replicated, may hold values from -0.25 to 0.25
- kernels: bfloat16 [16, 128, 128], replicated, may hold values from 0.049804688 to 1
- gain: float32 [512], replicated, may hold values from 0.1 to 1.9
- conv_weight: bfloat16 [3, 3, 512, 512], replicated, may hold values from -0.09375 to 0.09375
- cotangent: bfloat16 [192, 1024, 512], P('lat', 'lon'), may hold values from -6 to 6
Outputs:
- conv_out: bfloat16 [192, 1024, 512], P('lat', 'lon')
- conv_grad: float32 [3, 3, 512, 512], replicated
- encoder_grad: float32 [616, 512], replicated
- gain_grad: float32 [512], replicated
Inputs may be any that keep to these rules, and one draw needn't show every extreme that they name: `block_target`: within one device's 24 blocks no tile is named more than 3 times; in every latitude band one tile is named exactly 3 times by every device of the band.
All inputs are finite; a program needn't handle non-finite values.
Results may differ from a plain program's by a relative error of at most 0.0059.
Values may be sent and summed in bfloat16 or wider, within the bound.
A program may use at most 192 MiB of HBM per device.

v0:
```python
import math
import jax
import jax.numpy as jnp
from jax import lax
from jax.sharding import PartitionSpec as P

PH = 8
PW = 16
MOST = 3


def padded_2(shard, sides, width, wrap):
    for axis, dim in sides:
        size, length = (lax.axis_size(axis), shard.shape[dim])
        up = [(i, (i + 1) % size) for i in range(size if wrap else size - 1)]
        down = [(j, i) for i, j in up]
        last = lax.slice_in_dim(shard, length - width, length, axis=dim)
        leading = lax.slice_in_dim(shard, 0, width, axis=dim)
        before = lax.ppermute(last, axis, up)
        after = lax.ppermute(leading, axis, down)
        shard = jnp.concatenate([before, shard, after], axis=dim)
    return shard


def gather_turned(arrays, axis, dims):
    turned = [jnp.moveaxis(a, dim, 0) for a, dim in zip(arrays, dims)]
    both = jnp.concatenate([t.reshape(len(t), -1) for t in turned], axis=1)
    result, at, finished = (lax.all_gather(both, axis, axis=0, tiled=True), 0, [])
    for t, dim in zip(turned, dims):
        piece = result[:, at : at + t[0].size].reshape(-1, *t.shape[1:])
        finished.append(jnp.moveaxis(piece, 0, dim))
        at += t[0].size
    return tuple(finished)


def normalise(field, gain):
    meansq = jnp.mean(field * field, axis=-1, keepdims=True)
    return field * lax.rsqrt(meansq + 1e-06) * gain


def silu_slope(preact):
    logistic = jax.nn.sigmoid(preact)
    return logistic * (1.0 + preact * (1.0 - logistic))


def widen(field):
    beside_all = padded_2(field, (("lon", 1),), 1, True)
    return padded_2(beside_all, (("lat", 0),), 1, False)


def slot_layout(targets, lon_count):
    lanes = jnp.arange(lon_count, dtype=jnp.int32)
    onehot = (targets[..., None] == lanes).astype(jnp.int32)
    before = jnp.cumsum(onehot, axis=-2) - onehot
    ranks = jnp.sum(before * onehot, axis=-1)
    return targets * MOST + ranks


def to_tile(patches_in, tile_rows, tile_cols, width):
    shaped = patches_in.reshape(tile_rows // PH, tile_cols // PW, PH, PW, width)
    return shaped.transpose(0, 2, 1, 3, 4).reshape(tile_rows, tile_cols, width)


def to_patches(tile, tile_rows, tile_cols, width):
    shaped = tile.reshape(tile_rows // PH, PH, tile_cols // PW, PW, width)
    return shaped.transpose(0, 2, 1, 3, 4).reshape(-1, PH * PW, width)


def shards(
    spectra,
    block_target,
    block_patch,
    block_kernel,
    encoder_weight,
    kernels,
    gain,
    conv_weight,
    cotangent,
):
    lon_count = lax.axis_size("lon")
    lat_count = lax.axis_size("lat")
    own_lon = lax.axis_index("lon")
    blocks = block_target.shape[0]
    kernel_count, block_rows, patch_cells = kernels.shape
    channels = spectra.shape[1]
    width = encoder_weight.shape[1]
    tile_rows, tile_cols = (cotangent.shape[0], cotangent.shape[1])
    slots = lon_count * MOST
    patch_count = tile_rows // PH * (tile_cols // PW)
    loss_scale = 1.0 / math.sqrt(tile_rows * lat_count * tile_cols * lon_count)
    all_target, all_patch, all_kernel = gather_turned(
        (block_target, block_patch, block_kernel), "lon", (0, 0, 0)
    )
    all_target = all_target.reshape(lon_count, blocks)
    all_patch = all_patch.reshape(lon_count, blocks)
    all_kernel = all_kernel.reshape(lon_count, blocks)
    own_slot = slot_layout(block_target, lon_count)
    slot_ids = jnp.arange(slots, dtype=jnp.int32)
    chosen_slots = own_slot[None, :] == slot_ids[:, None]
    filled = jnp.any(chosen_slots, axis=1)
    source_block = jnp.sum(chosen_slots * jnp.arange(blocks, dtype=jnp.int32)[None, :], axis=1)
    all_slot = slot_layout(all_target, lon_count)
    wanted = own_lon * MOST + jnp.arange(MOST, dtype=jnp.int32)
    arrive = (all_slot[:, None, :] == wanted[None, :, None]).astype(jnp.int32)
    present = jnp.sum(arrive, axis=2).reshape(-1) > 0
    slot_kernel = jnp.sum(arrive * all_kernel[:, None, :], axis=2).reshape(-1)
    slot_kernel = jnp.where(present, slot_kernel, -1)
    slot_patch = jnp.sum(arrive * all_patch[:, None, :], axis=2).reshape(-1)
    taken = jnp.take(spectra.reshape(blocks, block_rows, channels), source_block, axis=0)
    taken = jnp.where(filled[:, None, None], taken, jnp.zeros_like(taken))
    arrived = lax.all_to_all(
        taken.reshape(lon_count, MOST, -1), "lon", split_axis=0, concat_axis=0, tiled=True
    )
    slot_spectra = arrived.reshape(slots * block_rows, channels)
    slot_preact = jnp.dot(slot_spectra, encoder_weight, preferred_element_type=jnp.float32)
    slot_rows = jax.nn.silu(slot_preact).astype(jnp.bfloat16).reshape(slots, block_rows, width)
    kernel_pick = (
        slot_kernel[:, None] == jnp.arange(kernel_count, dtype=jnp.int32)[None, :]
    ).astype(jnp.bfloat16)
    slot_kernels = jnp.dot(
        kernel_pick, kernels.reshape(kernel_count, -1), preferred_element_type=jnp.float32
    )
    slot_kernels = slot_kernels.astype(jnp.bfloat16).reshape(slots, block_rows, patch_cells)
    contribution = jnp.einsum(
        "sbp,sbd->spd", slot_kernels, slot_rows, preferred_element_type=jnp.float32
    )
    patch_pick = (slot_patch[:, None] == jnp.arange(patch_count, dtype=jnp.int32)[None, :]).astype(
        jnp.float32
    )
    tile_patches = jnp.einsum(
        "sq,spd->qpd", patch_pick, contribution, precision=lax.Precision.HIGHEST
    )
    spread = to_tile(tile_patches, tile_rows, tile_cols, width)
    normed = normalise(spread, gain).astype(jnp.bfloat16)
    padded = widen(normed)
    windows = []
    result_sum = jnp.zeros((tile_rows * tile_cols, width), jnp.float32)
    for row_shift in range(3):
        for col_shift in range(3):
            window = padded[
                row_shift : row_shift + tile_rows, col_shift : col_shift + tile_cols
            ].reshape(-1, width)
            windows.append(window)
            result_sum = result_sum + jnp.dot(
                window, conv_weight[row_shift, col_shift], preferred_element_type=jnp.float32
            )
    conv_out = result_sum.reshape(tile_rows, tile_cols, width).astype(jnp.bfloat16)
    cot_padded = widen(cotangent)
    cot_flat = cotangent.reshape(-1, width)
    d_normed = jnp.zeros((tile_rows * tile_cols, width), jnp.float32)
    kernel_grads = []
    for row_shift in range(3):
        for col_shift in range(3):
            back_window = cot_padded[
                2 - row_shift : 2 - row_shift + tile_rows, 2 - col_shift : 2 - col_shift + tile_cols
            ].reshape(-1, width)
            d_normed = d_normed + lax.dot_general(
                back_window,
                conv_weight[row_shift, col_shift],
                (((1,), (1,)), ((), ())),
                preferred_element_type=jnp.float32,
            )
            kernel_grads.append(
                lax.dot_general(
                    windows[row_shift * 3 + col_shift],
                    cot_flat,
                    (((0,), (0,)), ((), ())),
                    preferred_element_type=jnp.float32,
                )
            )
    conv_part = jnp.stack(kernel_grads).reshape(3, 3, width, width)
    _, pullback = jax.vjp(normalise, spread, gain)
    d_spread, gain_part = pullback(d_normed.reshape(tile_rows, tile_cols, width))
    d_patches = to_patches(d_spread.astype(jnp.bfloat16), tile_rows, tile_cols, width)
    slot_dpatch = jnp.take(d_patches, slot_patch, axis=0)
    slot_drows = jnp.einsum(
        "sbp,spd->sbd", slot_kernels, slot_dpatch, preferred_element_type=jnp.float32
    ).astype(jnp.bfloat16)
    d_preact = (slot_drows.reshape(-1, width).astype(jnp.float32) * silu_slope(slot_preact)).astype(
        jnp.bfloat16
    )
    encoder_part = lax.dot_general(
        slot_spectra, d_preact, (((0,), (0,)), ((), ())), preferred_element_type=jnp.float32
    )
    conv_total, encoder_total, gain_total = lax.psum(
        (conv_part, encoder_part, gain_part), ("lat", "lon")
    )
    return (conv_out, conv_total * loss_scale, encoder_total * loss_scale, gain_total * loss_scale)


def solution(mesh):
    placed = (
        P(("lat", "lon"), None),
        P(("lat", "lon")),
        P(("lat", "lon")),
        P(("lat", "lon")),
        P(),
        P(),
        P(),
        P(),
        P("lat", "lon", None),
    )
    return jax.shard_map(
        shards,
        mesh=mesh,
        in_specs=placed,
        out_specs=(P("lat", "lon", None), P(), P(), P()),
        check_vma=False,
    )
```

profile of v0, /device:TPU:1, one launch (start us, length us, event | category | flops | bytes accessed | tf_op | source)
XLA Modules:
  0.0 534.1 jit_solution(6251264387614628848)
XLA Ops:
  10.5 20.2 %all-gather = s32[16,24,3]{1,2,0:T(4,128)S(1)} all-gather(s32[1,24,3]{1,2,0:T(4,128)S(1)} %add_bitcast_fusion), channel_id=1, replica_groups=mesh['lat'=8,'lon'=16] {'lon'}, dimensions={0}, use_global_device_ids=true | all-gather | bytes 4896 | tf_op jit(solution)/shard_map/all_gather | solution.py:28
  32.4 4.6 copy_bitcast_fusion
  37.0 7.6 %gather_fusion = bf16[48,128,616]{1,2,0:T(8,128)(2,1)} fusion(bf16[24,128,616]{1,2,0:T(8,128)(2,1)} %copy_bitcast_fusion, s32[1024]{0:T(1024)S(1)} %get-tuple-element.49), kind=kCustom, calls=%fused_computation | custom fusion | bytes 15139008 | tf_op jit(solution)/shard_map/jit(_take)/gather | solution.py:109
  44.6 10.3 %copy.102 = bf16[48,128,616]{2,1,0:T(8,128)(2,1)} copy(bf16[48,128,616]{1,2,0:T(8,128)(2,1)} %gather_fusion) | data formatting | bytes 15138816 | tf_op jit(solution)/shard_map/jit(_take)/gather | solution.py:109
  54.9 20.1 %gather.11 = bf16[16,3,78848]{2,1,0:T(4,128)(2,1)} reshape(bf16[48,128,616]{2,1,0:T(8,128)(2,1)} %copy.102) | data formatting | bytes 15138816 | tf_op jit(solution)/shard_map/jit(_take)/gather | solution.py:109
  75.3 9.7 %select_select_fusion = bf16[16,3,78848]{2,1,0:T(4,128)(2,1)} fusion(bf16[16,3,78848]{2,1,0:T(4,128)(2,1)} %gather.11, pred[16,3]{1,0:T(8,128)(4,1)S(1)} %copy.100, pred[16,3]{1,0:T(8,128)(4,1)S(1)} %broadcast_in_dim.57), kind=kLoop, calls=%fused_computation.9 | loop fusion | flops 7569408 | bytes 15138912 | tf_op jit(solution)/shard_map/jit(_where)/select_n | solution.py:110
  85.0 5.0 all-to-all-start
  91.5 3.5 collective-permute-start.5
  99.6 104.8 %collective-permute-done.4 = bf16[24,1,512]{2,1,0:T(2,128)(2,1)S(1)} collective-permute-done((bf16[24,1,512]{2,1,0:T(2,128)(2,1)S(1)}, bf16[24,1,512]{2,1,0:T(2,128)(2,1)S(1)}, u32[]{:S(2)}, u32[]{:S(2)}) %collective-permute-start.4) | collective-permute-done | bytes 24608 | tf_op jit(solution)/shard_map/ppermute | solution.py:19
  204.5 5.4 %collective-permute-done.5 = bf16[24,1,512]{2,1,0:T(2,128)(2,1)S(1)} collective-permute-done((bf16[24,1,512]{2,1,0:T(2,128)(2,1)S(1)}, bf16[24,1,512]{2,1,0:T(2,128)(2,1)S(1)}, u32[]{:S(2)}, u32[]{:S(2)}) %collective-permute-start.5) | collective-permute-done | bytes 24608 | tf_op jit(solution)/shard_map/ppermute | solution.py:20
  210.0 8.4 %collective-permute-start.6 = (bf16[1,66,512]{2,1,0:T(8,128)(2,1)S(1)}, bf16[1,66,512]{2,1,0:T(8,128)(2,1)S(1)}, u32[]{:S(2)}, u32[]{:S(2)}) collective-permute-start(bf16[1,66,512]{2,1,0:T(8,128)(2,1)S(1)} %get-tuple-element.34), channel_id=1, source_target_pairs={{16,0},{32,16},{48,32},{64,48},{80,64},{96,80},{112,96},{17,1},{33... | collective-permute-start | bytes 202760 | tf_op jit(solution)/shard_map/ppermute | solution.py:20
  218.4 3.2 collective-permute-start.7
  224.8 2.3 fusion.96
  234.7 2.7 convolution_add_fusion
  237.4 20.1 %reshape.267 = bf16[6144,616]{1,0:T(8,128)(2,1)} reshape(bf16[16,3,78848]{2,1,0:T(4,128)(2,1)} %all-to-all-done) | data formatting | bytes 15138816 | tf_op jit(solution)/shard_map/reshape | solution.py:114
  257.5 11.7 %multiply_convert_fusion = (bf16[6144,512]{1,0:T(8,128)(2,1)S(1)}, f32[6144,512]{1,0:T(8,128)}) fusion(bf16[6144,616]{1,0:T(8,128)(2,1)} %reshape.267, bf16[616,512]{1,0:T(8,128)(2,1)S(1)} %copy-done), kind=kOutput, calls=%fused_computation.7 | convolution fusion | flops 3891265536 | bytes 27074560 | tf_op jit(solution)/shard_map/dot_general | solution.py:115
  271.1 12.0 %fusion.1 = f32[12,128,512]{2,0,1:T(8,128)S(1)} fusion(f32[48,128,512]{2,1,0:T(8,128)S(1)} %fusion.101, s32[48]{0:T(128)S(1)} %eq.86), kind=kOutput, calls=%fused_computation.5 | convolution fusion | flops 452985408 | bytes 15728832 | tf_op jit(solution)/shard_map/sq,spd->qpd/dot_general | solution.py:130
  294.4 4.8 collective-permute-start.1
  299.2 6.6 %gather_fusion.1 = bf16[48,128,512]{2,1,0:T(8,128)(2,1)} fusion(bf16[12,128,512]{2,1,0:T(8,128)(2,1)} %bitcast.199, s32[1024]{0:T(1024)S(1)} %get-tuple-element.48), kind=kCustom, calls=%fused_computation.1 | custom fusion | bytes 12583104 | tf_op jit(solution)/shard_map/jit(_take)/gather | solution.py:175
  305.7 5.3 fusion.6
  311.0 7.8 %fusion = bf16[6144,512]{1,0:T(8,128)(2,1)S(1)} fusion(f32[6144,512]{1,0:T(8,128)} %get-tuple-element.47, bf16[48,128,512]{2,1,0:T(8,128)(2,1)S(1)} %fusion.6), kind=kLoop, calls=%fused_computation.4 | loop fusion | flops 31457280 | bytes 25165824 | tf_op jit(solution)/shard_map/convert_element_type | solution.py:179
  318.8 5.1 fusion.102
  324.0 4.8 collective-permute-start.2
  332.0 2.6 collective-permute-done.3
  334.5 2.3 maximum_maximum_fusion
  346.1 3.7 copy-done.16
  350.0 2.9 copy.108
  352.8 2.3 fusion.15
  355.1 66.0 %psum.23 = f32[512]{0:T(512)S(1)} all-reduce(f32[512]{0:T(512)S(1)} %fusion.15), channel_id=1, replica_groups=mesh['lat'=8,'lon'=16] {'lat','lon'}, use_global_device_ids=true, to_apply=%region_14.15 | all-reduce | flops 512 | bytes 4096 | tf_op jit(solution)/shard_map/psum | solution.py:185
  421.7 2.6 fusion.43
  437.2 79.2 %all-reduce.3.cloned.1.call-done = (f32[3,3,512,512]{3,2,1,0:T(8,128)}, f32[616,512]{1,0:T(8,128)}) async-done(((f32[3,3,512,512]{3,2,1,0:T(8,128)}, f32[616,512]{1,0:T(8,128)}), (f32[3,3,512,512]{3,2,1,0:T(8,128)}, f32[616,512]{1,0:T(8,128)})) %all-reduce.3.cloned.1.call-update) | async-done | bytes 10698768 | tf_op jit(solution)/shard_map/psum | solution.py:185
  516.4 9.2 %broadcast_multiply_fusion = f32[3,3,512,512]{3,2,1,0:T(8,128)} fusion(f32[3,3,512,512]{3,2,1,0:T(8,128)} %get-tuple-element.12), kind=kLoop, calls=%fused_computation.14 | loop fusion | flops 2359296 | bytes 18874368 | tf_op jit(solution)/shard_map/mul | solution.py:188
  (147 shorter events, 62.1 us)
Async XLA Ops:
  7.2 250.3 %copy-start = (bf16[616,512]{1,0:T(8,128)(2,1)S(1)}, bf16[616,512]{1,0:T(8,128)(2,1)}, u32[]{:S(2)}) copy-start(bf16[616,512]{1,0:T(8,128)(2,1)} %param.13) | copy-start | bytes 1892356
  85.0 5.0 copy-start.2
  85.0 152.4 %all-to-all-start = ((bf16[16,3,78848]{2,1,0:T(4,128)(2,1)}), bf16[16,3,78848]{2,1,0:T(4,128)(2,1)}, u32[]{:S(2)}, u32[]{:S(2)}) async-start(bf16[16,3,78848]{2,1,0:T(4,128)(2,1)} %select_select_fusion), calls=%async_computation | async-start | bytes 20185088 | tf_op jit(solution)/shard_map/all_to_all | solution.py:111
  90.0 426.4 %all-reduce.3.cloned.1.call-start = ((), (), s32[]{:S(2)}) async-start(), calls=%async_computation.1 | async-start | bytes 21397504 | tf_op jit(solution)/shard_map/psum | solution.py:185
  90.2 114.3 %collective-permute-start.4 = (bf16[24,1,512]{2,1,0:T(2,128)(2,1)S(1)}, bf16[24,1,512]{2,1,0:T(2,128)(2,1)S(1)}, u32[]{:S(2)}, u32[]{:S(2)}) collective-permute-start(bf16[24,1,512]{2,1,0:T(2,128)(2,1)S(1)} %get-tuple-element.42), channel_id=1, source_target_pairs={{0,1},{1,2},{2,3},{3,4},{4,5},{5,6},{6,7},{7,8},{8,9},{9,10},{10,1... | collective-permute-start | bytes 73736 | tf_op jit(solution)/shard_map/ppermute | solution.py:19
  91.5 118.4 %collective-permute-start.5 = (bf16[24,1,512]{2,1,0:T(2,128)(2,1)S(1)}, bf16[24,1,512]{2,1,0:T(2,128)(2,1)S(1)}, u32[]{:S(2)}, u32[]{:S(2)}) collective-permute-start(bf16[24,1,512]{2,1,0:T(2,128)(2,1)S(1)} %get-tuple-element.43), channel_id=1, source_target_pairs={{1,0},{2,1},{3,2},{4,3},{5,4},{6,5},{7,6},{8,7},{9,8},{10,9},{11,1... | collective-permute-start | bytes 73736 | tf_op jit(solution)/shard_map/ppermute | solution.py:20
  95.3 2.2 copy-start.18
  210.0 12.7 %collective-permute-start.6 = (bf16[1,66,512]{2,1,0:T(8,128)(2,1)S(1)}, bf16[1,66,512]{2,1,0:T(8,128)(2,1)S(1)}, u32[]{:S(2)}, u32[]{:S(2)}) collective-permute-start(bf16[1,66,512]{2,1,0:T(8,128)(2,1)S(1)} %get-tuple-element.34), channel_id=1, source_target_pairs={{16,0},{32,16},{48,32},{64,48},{80,64},{96,80},{112,96},{17,1},{33... | collective-permute-start | bytes 202760 | tf_op jit(solution)/shard_map/ppermute | solution.py:20
  218.4 4.4 collective-permute-start.7
  222.8 4.4 slice-start
  224.8 2.4 slice-start.1
  257.5 11.7 %copy-start.9 = (bf16[6,8,128,128]{3,2,1,0:T(8,128)(2,1)S(1)}, bf16[6,8,128,128]{3,2,1,0:T(8,128)(2,1)}, u32[]{:S(2)}) copy-start(bf16[6,8,128,128]{3,2,1,0:T(8,128)(2,1)} %copy.116) | copy-start | bytes 4718596
  284.9 3.0 copy-start.3
  284.9 3.0 copy-start.19
  294.3 29.6 %collective-permute-start = (bf16[24,1,512]{2,1,0:T(2,128)(2,1)S(1)}, bf16[24,1,512]{2,1,0:T(2,128)(2,1)S(1)}, u32[]{:S(2)}, u32[]{:S(2)}) collective-permute-start(bf16[24,1,512]{2,1,0:T(2,128)(2,1)S(1)} %get-tuple-element.38), channel_id=1, source_target_pairs={{0,1},{1,2},{2,3},{3,4},{4,5},{5,6},{6,7},{7,8},{8,9},{9,10},{10,1... | collective-permute-start | bytes 73736 | tf_op jit(solution)/shard_map/ppermute | solution.py:19
  294.4 29.6 %collective-permute-start.1 = (bf16[24,1,512]{2,1,0:T(2,128)(2,1)S(1)}, bf16[24,1,512]{2,1,0:T(2,128)(2,1)S(1)}, u32[]{:S(2)}, u32[]{:S(2)}) collective-permute-start(bf16[24,1,512]{2,1,0:T(2,128)(2,1)S(1)} %get-tuple-element.39), channel_id=1, source_target_pairs={{1,0},{2,1},{3,2},{4,3},{5,4},{6,5},{7,6},{8,7},{9,8},{10,9},{11,1... | collective-permute-start | bytes 73736 | tf_op jit(solution)/shard_map/ppermute | solution.py:20
  305.7 13.0 %slice-start.4 = ((s8[7864320]{0:T(1024)(128)(4,1)}), s8[4194304]{0:T(1024)(128)(4,1)S(1)}, s32[]{:S(2)}) async-start(s8[7864320]{0:T(1024)(128)(4,1)} %bitcast.216), calls=%async_computation.6 | async-start | bytes 8388608
  311.0 7.8 %slice-start.5 = ((s8[7864320]{0:T(1024)(128)(4,1)}), s8[3670016]{0:T(1024)(128)(4,1)S(1)}, s32[]{:S(2)}) async-start(s8[7864320]{0:T(1024)(128)(4,1)} %bitcast.216), calls=%async_computation.7 | async-start | bytes 7340032
  318.8 5.2 copy-start.6
  324.0 7.9 %collective-permute-start.2 = (bf16[1,66,512]{2,1,0:T(8,128)(2,1)S(1)}, bf16[1,66,512]{2,1,0:T(8,128)(2,1)S(1)}, u32[]{:S(2)}, u32[]{:S(2)}) collective-permute-start(bf16[1,66,512]{2,1,0:T(8,128)(2,1)S(1)} %get-tuple-element.30), channel_id=1, source_target_pairs={{0,16},{16,32},{32,48},{48,64},{64,80},{80,96},{96,112},{1,17},{17... | collective-permute-start | bytes 202760 | tf_op jit(solution)/shard_map/ppermute | solution.py:19
  328.9 5.7 %collective-permute-start.3 = (bf16[1,66,512]{2,1,0:T(8,128)(2,1)S(1)}, bf16[1,66,512]{2,1,0:T(8,128)(2,1)S(1)}, u32[]{:S(2)}, u32[]{:S(2)}) collective-permute-start(bf16[1,66,512]{2,1,0:T(8,128)(2,1)S(1)} %get-tuple-element.31), channel_id=1, source_target_pairs={{16,0},{32,16},{48,32},{64,48},{80,64},{96,80},{112,96},{17,1},{33... | collective-permute-start | bytes 202760 | tf_op jit(solution)/shard_map/ppermute | solution.py:20
  331.9 8.0 %copy-start.14 = (bf16[24,64,512]{2,1,0:T(8,128)(2,1)}, bf16[24,64,512]{2,1,0:T(8,128)(2,1)S(1)}, u32[]{:S(2)}) copy-start(bf16[24,64,512]{2,1,0:T(8,128)(2,1)S(1)} %get-tuple-element.37) | copy-start | bytes 4718596
  331.9 10.0 %copy-start.12 = (bf16[24,64,512]{2,1,0:T(8,128)(2,1)}, bf16[24,64,512]{2,1,0:T(8,128)(2,1)S(1)}, u32[]{:S(2)}) copy-start(bf16[24,64,512]{2,1,0:T(8,128)(2,1)S(1)} %get-tuple-element.36) | copy-start | bytes 4718596
  336.8 2.1 copy-start.10
  336.8 8.2 %copy-start.7 = (bf16[25,66,512]{2,1,0:T(8,128)(2,1)}, bf16[25,66,512]{2,1,0:T(8,128)(2,1)S(1)}, u32[]{:S(2)}) copy-start(bf16[25,66,512]{2,1,0:T(8,128)(2,1)S(1)} %get-tuple-element.29) | copy-start | bytes 5068804
  346.1 3.7 copy-start.16
  349.8 3.0 copy-start.4
  421.7 2.6 copy-start.11
  421.7 3.8 slice-start.2
  425.6 1.5 copy-start.8
  516.4 9.2 %copy-start.17 = (f32[616,512]{1,0:T(8,128)S(1)}, f32[616,512]{1,0:T(8,128)}, u32[]{:S(2)}) copy-start(f32[616,512]{1,0:T(8,128)} %get-tuple-element.13) | copy-start | bytes 3784708
  516.4 10.4 %copy-start.1 = (bf16[616,512]{1,0:T(8,128)(2,1)S(1)}, bf16[616,512]{1,0:T(8,128)(2,1)}, u32[]{:S(2)}) copy-start(bf16[616,512]{1,0:T(8,128)(2,1)} %param.13) | copy-start | bytes 1892356
  (4 other events, 5.2 us)
Sparse Core Ops, SparseCore 0:
  350.0 166.4 all-reduce.2
where the time goes:
time: 542 us; the launch traced here: 534 us
  waiting for transfers between devices  192 us (35%)
  local copies, waits for them, and re-layouts  91 us (17%)
  blocking collectives  86.2 us (16%)
  matrix products  69.9 us (13%)
  other arithmetic  46.6 us (9%)
  starting transfers between devices  33.1 us (6%)
  between operations  15.2 us (3%)
    ppermute x4, waiting for transfers between devices, padded_2(): before = lax.ppermute(last, axis, up)  105 us
    psum x1, waiting for transfers between devices, shards(): lax.psum((conv_part, encoder_part, gain_part), ('lat', 'lon'))  79.2 us
    psum x1, blocking collectives, shards(): lax.psum((conv_part, encoder_part, gain_part), ('lat', 'lon'))  66 us
    gather x3, local copies, waits for them, and re-layouts, shards(): jnp.take(spectra.reshape(blocks, block_rows, channels), source_block, axi...  38 us
    all_gather x1, blocking collectives, gather_turned(): lax.all_gather(both, axis, axis=0, tiled=True)  20.2 us
    reshape x1, local copies, waits for them, and re-layouts, shards(): slot_spectra = arrived.reshape(slots * block_rows, channels)  20.1 us
    ppermute x4, starting transfers between devices, padded_2(): after = lax.ppermute(leading, axis, down)  18.6 us
    dot_general x9, matrix products, shards(): lax.dot_general(back_window, conv_weight[row_shift, col_shift], (((1,), (...  12.3 us
  transfers between devices with their start and end apart: 10, of which 5 were waited for; matrix products, arithmetic and copies ran while one was open for 12% of the time, Pallas kernels for 0%

commit v1 on v0

--- a/solution.py
+++ b/solution.py
@@ -25,7 +25,13 @@
 def gather_turned(arrays, axis, dims):
     turned = [jnp.moveaxis(a, dim, 0) for a, dim in zip(arrays, dims)]
     both = jnp.concatenate([t.reshape(len(t), -1) for t in turned], axis=1)
-    result, at, finished = (lax.all_gather(both, axis, axis=0, tiled=True), 0, [])
+    result, at, finished = (
+        jnp.concatenate(
+            lax.all_to_all(jnp.stack([both] * lax.axis_size(axis)), axis, 0, 0), axis=0
+        ),
+        0,
+        [],
+    )
     for t, dim in zip(turned, dims):
         piece = result[:, at : at + t[0].size].reshape(-1, *t.shape[1:])
         finished.append(jnp.moveaxis(piece, 0, dim))

time: 542 us -> 586 us (1.081)
  waiting for transfers between devices: 192 us -> 219 us
  starting transfers between devices: 33.1 us -> 43.1 us
    psum x1, blocking collectives: 66 us -> 89.7 us  [shards(): lax.psum((conv_part, encoder_part, gain_part), ('lat', 'lon'))]
    all_to_all x1, waiting for transfers between devices: 0.01 us -> 23.5 us  [shards(): lax.all_to_all(taken.reshape(lon_count, MOST, -1), 'lon', split_axis=0, c...]
    all_gather x1 -> x0, blocking collectives: 20.2 us -> none  [gather_turned(): lax.all_gather(both, axis, axis=0, tiled=True)]
    all_to_all x0 -> x1, starting transfers between devices: none -> 8.59 us  [gather_turned(): lax.all_to_all(jnp.stack([both] * lax.axis_size(axis)), axis, 0, 0)]
  transfers between devices with their start and end apart: 10 -> 11, of which waited for: 5 -> 6; matrix products, arithmetic and copies ran while one was open for 12% -> 13% of each run, Pallas kernels for 0% -> 0%
where the time goes in v1:
time: 586 us; the launch traced here: 578 us
  waiting for transfers between devices  219 us (37%)
  local copies, waits for them, and re-layouts  92.4 us (16%)
  blocking collectives  89.7 us (15%)
  matrix products  71.5 us (12%)
  other arithmetic  46.6 us (8%)
  starting transfers between devices  43.1 us (7%)
  between operations  15.2 us (3%)
    ppermute x4, waiting for transfers between devices, padded_2(): before = lax.ppermute(last, axis, up)  109 us
    psum x1, blocking collectives, shards(): lax.psum((conv_part, encoder_part, gain_part), ('lat', 'lon'))  89.7 us
    psum x1, waiting for transfers between devices, shards(): lax.psum((conv_part, encoder_part, gain_part), ('lat', 'lon'))  79.3 us
    gather x3, local copies, waits for them, and re-layouts, shards(): jnp.take(spectra.reshape(blocks, block_rows, channels), source_block, axi...  38 us
    all_to_all x1, waiting for transfers between devices, shards(): lax.all_to_all(taken.reshape(lon_count, MOST, -1), 'lon', split_axis=0, c...  23.5 us
    reshape x1, local copies, waits for them, and re-layouts, shards(): slot_spectra = arrived.reshape(slots * block_rows, channels)  20.1 us
    ppermute x4, starting transfers between devices, padded_2(): after = lax.ppermute(leading, axis, down)  15.2 us
    dot_general x9, matrix products, shards(): lax.dot_general(back_window, conv_weight[row_shift, col_shift], (((1,), (...  13.8 us
  transfers between devices with their start and end apart: 11, of which 6 were waited for; matrix products, arithmetic and copies ran while one was open for 13% of the time, Pallas kernels for 0%

profile of v1, /device:TPU:1, one launch (start us, length us, event | category | flops | bytes accessed | tf_op | source)
XLA Modules:
  0.0 577.5 jit_solution(634173661317245751)
XLA Ops:
  8.6 8.6 %all-to-all-start = ((s32[16,24,3]{1,2,0:T(4,128)}), s32[16,24,3]{1,2,0:T(4,128)S(1)}, u32[]{:S(2)}, u32[]{:S(2)}) async-start(s32[16,24,3]{1,2,0:T(4,128)} %stack.22), calls=%async_computation | async-start | bytes 65536 | tf_op jit(solution)/shard_map/all_to_all | solution.py:30
  19.7 4.6 copy_bitcast_fusion
  26.4 7.6 %gather_fusion = bf16[48,128,616]{1,2,0:T(8,128)(2,1)} fusion(bf16[24,128,616]{1,2,0:T(8,128)(2,1)} %copy_bitcast_fusion, s32[1024]{0:T(1024)S(1)} %get-tuple-element.49), kind=kCustom, calls=%fused_computation | custom fusion | bytes 15139008 | tf_op jit(solution)/shard_map/jit(_take)/gather | solution.py:115
  33.9 10.3 %copy.100 = bf16[48,128,616]{2,1,0:T(8,128)(2,1)} copy(bf16[48,128,616]{1,2,0:T(8,128)(2,1)} %gather_fusion) | data formatting | bytes 15138816 | tf_op jit(solution)/shard_map/jit(_take)/gather | solution.py:115
  44.2 20.1 %gather.11 = bf16[16,3,78848]{2,1,0:T(4,128)(2,1)} reshape(bf16[48,128,616]{2,1,0:T(8,128)(2,1)} %copy.100) | data formatting | bytes 15138816 | tf_op jit(solution)/shard_map/jit(_take)/gather | solution.py:115
  64.3 9.7 %select_select_fusion = bf16[16,3,78848]{2,1,0:T(4,128)(2,1)} fusion(bf16[16,3,78848]{2,1,0:T(4,128)(2,1)} %gather.11, pred[16,3]{1,0:T(8,128)(4,1)S(1)} %copy.98, pred[16,3]{1,0:T(8,128)(4,1)S(1)} %broadcast_in_dim.57), kind=kLoop, calls=%fused_computation.9 | loop fusion | flops 7569408 | bytes 15138912 | tf_op jit(solution)/shard_map/jit(_where)/select_n | solution.py:116
  74.0 6.9 %all-to-all-start.1 = ((bf16[16,3,78848]{2,1,0:T(4,128)(2,1)}), bf16[16,3,78848]{2,1,0:T(4,128)(2,1)}, u32[]{:S(2)}, u32[]{:S(2)}) async-start(bf16[16,3,78848]{2,1,0:T(4,128)(2,1)} %select_select_fusion), calls=%async_computation.1 | async-start | bytes 20185088 | tf_op jit(solution)/shard_map/all_to_all | solution.py:117
  82.4 3.5 collective-permute-start.5
  85.9 3.8 fusion.41
  92.2 108.9 %collective-permute-done.4 = bf16[24,1,512]{2,1,0:T(2,128)(2,1)S(1)} collective-permute-done((bf16[24,1,512]{2,1,0:T(2,128)(2,1)S(1)}, bf16[24,1,512]{2,1,0:T(2,128)(2,1)S(1)}, u32[]{:S(2)}, u32[]{:S(2)}) %collective-permute-start.4) | collective-permute-done | bytes 24608 | tf_op jit(solution)/shard_map/ppermute | solution.py:19
  201.1 4.6 collective-permute-done.5
  205.7 5.0 collective-permute-start.6
  210.8 3.5 collective-permute-start.7
  217.5 2.3 fusion.96
  228.1 2.7 convolution_add_fusion
  230.9 23.5 %all-to-all-done.1 = bf16[16,3,78848]{2,1,0:T(4,128)(2,1)} async-done(((bf16[16,3,78848]{2,1,0:T(4,128)(2,1)}), bf16[16,3,78848]{2,1,0:T(4,128)(2,1)}, u32[]{:S(2)}, u32[]{:S(2)}) %all-to-all-start.1) | async-done | bytes 7569440 | tf_op jit(solution)/shard_map/all_to_all | solution.py:117
  254.4 20.1 %reshape.273 = bf16[6144,616]{1,0:T(8,128)(2,1)} reshape(bf16[16,3,78848]{2,1,0:T(4,128)(2,1)} %all-to-all-done.1) | data formatting | bytes 15138816 | tf_op jit(solution)/shard_map/reshape | solution.py:120
  274.5 11.7 %multiply_convert_fusion = (bf16[6144,512]{1,0:T(8,128)(2,1)S(1)}, f32[6144,512]{1,0:T(8,128)}) fusion(bf16[6144,616]{1,0:T(8,128)(2,1)} %reshape.273, bf16[616,512]{1,0:T(8,128)(2,1)S(1)} %copy-done), kind=kOutput, calls=%fused_computation.7 | convolution fusion | flops 3891265536 | bytes 27074560 | tf_op jit(solution)/shard_map/dot_general | solution.py:121
  288.1 12.0 %fusion.1 = f32[12,128,512]{2,0,1:T(8,128)S(1)} fusion(f32[48,128,512]{2,1,0:T(8,128)S(1)} %fusion.101, s32[48]{0:T(128)S(1)} %eq.86), kind=kOutput, calls=%fused_computation.5 | convolution fusion | flops 452985408 | bytes 15728832 | tf_op jit(solution)/shard_map/sq,spd->qpd/dot_general | solution.py:136
  311.5 4.8 collective-permute-start.1
  316.2 6.6 %gather_fusion.1 = bf16[48,128,512]{2,1,0:T(8,128)(2,1)} fusion(bf16[12,128,512]{2,1,0:T(8,128)(2,1)} %bitcast.197, s32[1024]{0:T(1024)S(1)} %get-tuple-element.48), kind=kCustom, calls=%fused_computation.1 | custom fusion | bytes 12583104 | tf_op jit(solution)/shard_map/jit(_take)/gather | solution.py:181
  322.8 5.3 fusion.6
  328.1 7.8 %fusion = bf16[6144,512]{1,0:T(8,128)(2,1)S(1)} fusion(f32[6144,512]{1,0:T(8,128)} %get-tuple-element.47, bf16[48,128,512]{2,1,0:T(8,128)(2,1)S(1)} %fusion.6), kind=kLoop, calls=%fused_computation.4 | loop fusion | flops 31457280 | bytes 25165824 | tf_op jit(solution)/shard_map/convert_element_type | solution.py:185
  335.9 5.1 fusion.102
  341.1 7.4 %collective-permute-start.2 = (bf16[1,66,512]{2,1,0:T(8,128)(2,1)S(1)}, bf16[1,66,512]{2,1,0:T(8,128)(2,1)S(1)}, u32[]{:S(2)}, u32[]{:S(2)}) collective-permute-start(bf16[1,66,512]{2,1,0:T(8,128)(2,1)S(1)} %get-tuple-element.30), channel_id=1, source_target_pairs={{0,16},{16,32},{32,48},{48,64},{64,80},{80,96},{96,112},{1,17},{17... | collective-permute-start | bytes 202760 | tf_op jit(solution)/shard_map/ppermute | solution.py:19
  351.6 2.6 collective-permute-done.3
  365.7 3.7 copy-done.17
  369.6 2.9 copy.106
  374.7 89.7 %psum.23 = f32[512]{0:T(512)S(1)} all-reduce(f32[512]{0:T(512)S(1)} %fusion.15), channel_id=1, replica_groups=mesh['lat'=8,'lon'=16] {'lat','lon'}, use_global_device_ids=true, to_apply=%region_14.15 | all-reduce | flops 512 | bytes 4096 | tf_op jit(solution)/shard_map/psum | solution.py:191
  465.0 2.6 fusion.43
  480.5 79.3 %all-reduce.3.cloned.1.call-done = (f32[3,3,512,512]{3,2,1,0:T(8,128)}, f32[616,512]{1,0:T(8,128)}) async-done(((f32[3,3,512,512]{3,2,1,0:T(8,128)}, f32[616,512]{1,0:T(8,128)}), (f32[3,3,512,512]{3,2,1,0:T(8,128)}, f32[616,512]{1,0:T(8,128)})) %all-reduce.3.cloned.1.call-update) | async-done | bytes 10698768 | tf_op jit(solution)/shard_map/psum | solution.py:191
  559.8 9.2 %broadcast_multiply_fusion = f32[3,3,512,512]{3,2,1,0:T(8,128)} fusion(f32[3,3,512,512]{3,2,1,0:T(8,128)} %get-tuple-element.12), kind=kLoop, calls=%fused_computation.14 | loop fusion | flops 2359296 | bytes 18874368 | tf_op jit(solution)/shard_map/mul | solution.py:194
  (151 shorter events, 65.9 us)
Async XLA Ops:
  7.2 267.4 %copy-start = (bf16[616,512]{1,0:T(8,128)(2,1)S(1)}, bf16[616,512]{1,0:T(8,128)(2,1)}, u32[]{:S(2)}) copy-start(bf16[616,512]{1,0:T(8,128)(2,1)} %param.13) | copy-start | bytes 1892356
  8.6 16.0 %all-to-all-start = ((s32[16,24,3]{1,2,0:T(4,128)}), s32[16,24,3]{1,2,0:T(4,128)S(1)}, u32[]{:S(2)}, u32[]{:S(2)}) async-start(s32[16,24,3]{1,2,0:T(4,128)} %stack.22), calls=%async_computation | async-start | bytes 65536 | tf_op jit(solution)/shard_map/all_to_all | solution.py:30
  74.0 6.9 %copy-start.2 = (bf16[24,64,512]{2,1,0:T(8,128)(2,1)S(1)}, bf16[24,64,512]{2,1,0:T(8,128)(2,1)}, u32[]{:S(2)}) copy-start(bf16[24,64,512]{2,1,0:T(8,128)(2,1)} %param.17) | copy-start | bytes 4718596
  74.0 180.4 %all-to-all-start.1 = ((bf16[16,3,78848]{2,1,0:T(4,128)(2,1)}), bf16[16,3,78848]{2,1,0:T(4,128)(2,1)}, u32[]{:S(2)}, u32[]{:S(2)}) async-start(bf16[16,3,78848]{2,1,0:T(4,128)(2,1)} %select_select_fusion), calls=%async_computation.1 | async-start | bytes 20185088 | tf_op jit(solution)/shard_map/all_to_all | solution.py:117
  80.9 478.9 %all-reduce.3.cloned.1.call-start = ((), (), s32[]{:S(2)}) async-start(), calls=%async_computation.2 | async-start | bytes 21397504 | tf_op jit(solution)/shard_map/psum | solution.py:191
  81.1 120.0 %collective-permute-start.4 = (bf16[24,1,512]{2,1,0:T(2,128)(2,1)S(1)}, bf16[24,1,512]{2,1,0:T(2,128)(2,1)S(1)}, u32[]{:S(2)}, u32[]{:S(2)}) collective-permute-start(bf16[24,1,512]{2,1,0:T(2,128)(2,1)S(1)} %get-tuple-element.42), channel_id=1, source_target_pairs={{0,1},{1,2},{2,3},{3,4},{4,5},{5,6},{6,7},{7,8},{8,9},{9,10},{10,1... | collective-permute-start | bytes 73736 | tf_op jit(solution)/shard_map/ppermute | solution.py:19
  82.4 123.2 %collective-permute-start.5 = (bf16[24,1,512]{2,1,0:T(2,128)(2,1)S(1)}, bf16[24,1,512]{2,1,0:T(2,128)(2,1)S(1)}, u32[]{:S(2)}, u32[]{:S(2)}) collective-permute-start(bf16[24,1,512]{2,1,0:T(2,128)(2,1)S(1)} %get-tuple-element.43), channel_id=1, source_target_pairs={{1,0},{2,1},{3,2},{4,3},{5,4},{6,5},{7,6},{8,7},{9,8},{10,9},{11,1... | collective-permute-start | bytes 73736 | tf_op jit(solution)/shard_map/ppermute | solution.py:20
  85.9 4.1 copy-start.19
  205.7 9.7 %collective-permute-start.6 = (bf16[1,66,512]{2,1,0:T(8,128)(2,1)S(1)}, bf16[1,66,512]{2,1,0:T(8,128)(2,1)S(1)}, u32[]{:S(2)}, u32[]{:S(2)}) collective-permute-start(bf16[1,66,512]{2,1,0:T(8,128)(2,1)S(1)} %get-tuple-element.34), channel_id=1, source_target_pairs={{16,0},{32,16},{48,32},{64,48},{80,64},{96,80},{112,96},{17,1},{33... | collective-permute-start | bytes 202760 | tf_op jit(solution)/shard_map/ppermute | solution.py:20
  210.8 4.7 collective-permute-start.7
  215.5 4.4 slice-start
  217.5 2.4 slice-start.1
  274.5 11.7 %copy-start.10 = (bf16[6,8,128,128]{3,2,1,0:T(8,128)(2,1)S(1)}, bf16[6,8,128,128]{3,2,1,0:T(8,128)(2,1)}, u32[]{:S(2)}) copy-start(bf16[6,8,128,128]{3,2,1,0:T(8,128)(2,1)} %copy.114) | copy-start | bytes 4718596
  302.0 3.0 copy-start.3
  302.0 3.0 copy-start.20
  311.4 29.6 %collective-permute-start = (bf16[24,1,512]{2,1,0:T(2,128)(2,1)S(1)}, bf16[24,1,512]{2,1,0:T(2,128)(2,1)S(1)}, u32[]{:S(2)}, u32[]{:S(2)}) collective-permute-start(bf16[24,1,512]{2,1,0:T(2,128)(2,1)S(1)} %get-tuple-element.38), channel_id=1, source_target_pairs={{0,1},{1,2},{2,3},{3,4},{4,5},{5,6},{6,7},{7,8},{8,9},{9,10},{10,1... | collective-permute-start | bytes 73736 | tf_op jit(solution)/shard_map/ppermute | solution.py:19
  311.5 29.6 %collective-permute-start.1 = (bf16[24,1,512]{2,1,0:T(2,128)(2,1)S(1)}, bf16[24,1,512]{2,1,0:T(2,128)(2,1)S(1)}, u32[]{:S(2)}, u32[]{:S(2)}) collective-permute-start(bf16[24,1,512]{2,1,0:T(2,128)(2,1)S(1)} %get-tuple-element.39), channel_id=1, source_target_pairs={{1,0},{2,1},{3,2},{4,3},{5,4},{6,5},{7,6},{8,7},{9,8},{10,9},{11,1... | collective-permute-start | bytes 73736 | tf_op jit(solution)/shard_map/ppermute | solution.py:20
  322.8 13.0 %slice-start.4 = ((s8[7864320]{0:T(1024)(128)(4,1)}), s8[4194304]{0:T(1024)(128)(4,1)S(1)}, s32[]{:S(2)}) async-start(s8[7864320]{0:T(1024)(128)(4,1)} %bitcast.214), calls=%async_computation.7 | async-start | bytes 8388608
  328.1 7.8 %slice-start.5 = ((s8[7864320]{0:T(1024)(128)(4,1)}), s8[3670016]{0:T(1024)(128)(4,1)S(1)}, s32[]{:S(2)}) async-start(s8[7864320]{0:T(1024)(128)(4,1)} %bitcast.214), calls=%async_computation.8 | async-start | bytes 7340032
  335.9 5.2 copy-start.6
  341.1 10.5 %collective-permute-start.2 = (bf16[1,66,512]{2,1,0:T(8,128)(2,1)S(1)}, bf16[1,66,512]{2,1,0:T(8,128)(2,1)S(1)}, u32[]{:S(2)}, u32[]{:S(2)}) collective-permute-start(bf16[1,66,512]{2,1,0:T(8,128)(2,1)S(1)} %get-tuple-element.30), channel_id=1, source_target_pairs={{0,16},{16,32},{32,48},{48,64},{64,80},{80,96},{96,112},{1,17},{17... | collective-permute-start | bytes 202760 | tf_op jit(solution)/shard_map/ppermute | solution.py:19
  348.5 5.7 collective-permute-start.3
  351.6 8.0 %copy-start.15 = (bf16[24,64,512]{2,1,0:T(8,128)(2,1)}, bf16[24,64,512]{2,1,0:T(8,128)(2,1)S(1)}, u32[]{:S(2)}) copy-start(bf16[24,64,512]{2,1,0:T(8,128)(2,1)S(1)} %get-tuple-element.37) | copy-start | bytes 4718596
  351.6 10.0 %copy-start.13 = (bf16[24,64,512]{2,1,0:T(8,128)(2,1)}, bf16[24,64,512]{2,1,0:T(8,128)(2,1)S(1)}, u32[]{:S(2)}) copy-start(bf16[24,64,512]{2,1,0:T(8,128)(2,1)S(1)} %get-tuple-element.36) | copy-start | bytes 4718596
  356.5 2.1 copy-start.11
  356.5 8.2 %copy-start.7 = (bf16[25,66,512]{2,1,0:T(8,128)(2,1)}, bf16[25,66,512]{2,1,0:T(8,128)(2,1)S(1)}, u32[]{:S(2)}) copy-start(bf16[25,66,512]{2,1,0:T(8,128)(2,1)S(1)} %get-tuple-element.29) | copy-start | bytes 5068804
  365.7 3.7 copy-start.17
  369.5 3.0 copy-start.4
  465.0 2.6 copy-start.12
  465.0 3.8 slice-start.2
  559.8 9.2 %copy-start.18 = (f32[616,512]{1,0:T(8,128)S(1)}, f32[616,512]{1,0:T(8,128)}, u32[]{:S(2)}) copy-start(f32[616,512]{1,0:T(8,128)} %get-tuple-element.13) | copy-start | bytes 3784708
  559.8 10.4 %copy-start.1 = (bf16[616,512]{1,0:T(8,128)(2,1)S(1)}, bf16[616,512]{1,0:T(8,128)(2,1)}, u32[]{:S(2)}) copy-start(bf16[616,512]{1,0:T(8,128)(2,1)} %param.13) | copy-start | bytes 1892356
  (6 other events, 8.6 us)
Sparse Core Ops, SparseCore 0:
  369.6 190.1 all-reduce.2
